TPU v7x, 128 devices: a whole 4x4x4 slice. The times are simulated.
128 devices in a mesh: row: 16 (over x, y), col: 8 (over z, core).
Axes of the slice: x: 4, y: 4, z: 4, core: 2. Of those that a mesh axis runs over, the one named last changes fastest.
Arguments:
- activations: bfloat16 [1024, 28672], P('row', 'col'), may hold values from -6 to 6
- act_basis: bfloat16 [28672, 28672], P('col', 'row'), may hold values from -0.03125 to 0.03125
- grads: bfloat16 [1024, 8192], P('col', 'row'), may hold values from -6 to 6
- grad_basis: bfloat16 [8192, 8192], P('row', 'col'), may hold values from -0.0625 to 0.0625
Outputs:
- eigenvalues: float32 [28672, 8192], P('row', 'col')
All inputs are finite; a program needn't handle non-finite values.
Results may differ from a plain program's by a relative error of at most 0.0034.
Values may be sent and summed in bfloat16 or wider, within the bound.
A program may use at most 128 MiB of HBM per device.

v0:
```python
import math

import jax
import jax.numpy as jnp
from jax import lax
from jax.sharding import PartitionSpec as P

SEQS = 4
LEN = 256


def in_order(pieces, dim):
    pieces = jnp.moveaxis(pieces, 0, dim)
    dims = pieces.shape
    return pieces.reshape(*dims[:dim], dims[dim] * dims[dim + 1], *dims[dim + 2 :])


def sent_to_all(shard, axis):
    copies = jnp.broadcast_to(shard, (lax.axis_size(axis), *shard.shape))
    return lax.all_to_all(copies, axis, split_axis=0, concat_axis=0, tiled=True)


def gathered_copies(shard, axis, dim):
    return in_order(sent_to_all(shard, axis), dim)


def shards(activations, act_basis, grads, grad_basis):
    tokens_all = lax.all_gather(activations, "row", axis=0, tiled=True)
    partial_acts = jnp.dot(tokens_all, act_basis, preferred_element_type=jnp.float32)
    rotated_acts = lax.psum(partial_acts, "col").astype(jnp.bfloat16)
    partial_grads = jnp.dot(
        gathered_copies(grads, "col", 0), grad_basis, preferred_element_type=jnp.float32
    )
    rotated_grads = lax.psum(partial_grads, "row").astype(jnp.bfloat16)
    scale = 1.0 / math.sqrt(LEN)
    total = jnp.zeros((rotated_acts.shape[1], rotated_grads.shape[1]), jnp.float32)
    for seq_index in range(SEQS):
        left = rotated_acts[seq_index * LEN : (seq_index + 1) * LEN]
        right = rotated_grads[seq_index * LEN : (seq_index + 1) * LEN]
        products = (
            lax.dot_general(
                left, right, (((0,), (0,)), ((), ())), preferred_element_type=jnp.float32
            )
            * scale
        )
        total = total + products * products
    return total / SEQS


def solution(mesh):
    return jax.shard_map(
        shards,
        mesh=mesh,
        in_specs=(P("row", "col"), P("col", "row"), P("col", "row"), P("row", "col")),
        out_specs=P("row", "col"),
        check_vma=False,
    )
```

profile of v0, /device:TPU:1, one launch (start us, length us, event | category | flops | bytes accessed | tf_op | source)
XLA Modules:
  0.0 289.3 jit_solution(16143040985152910441)
XLA Ops:
  6.5 0.0 copy-start
  6.5 0.0 all-gather.2.cloned.1.call-start
  6.5 0.7 all-gather.2.cloned.1.call-update
  7.3 1.0 broadcast_in_dim.3
  8.3 21.6 %all_to_all.5 = bf16[8,128,512]{2,1,0:T(8,128)(2,1)S(1)} all-to-all(bf16[8,128,512]{2,1,0:T(8,128)(2,1)S(1)} %broadcast_in_dim.3), channel_id=1, replica_groups=mesh['row'=16,'col'=8] {'col'}, dimensions={0} | all-to-all | bytes 2097152 | tf_op jit(solution)/shard_map/all_to_all | solution.py:20
  29.8 0.0 copy-done
  29.9 3.3 %fusion.12 = f32[1024,1024]{1,0:T(8,128)} fusion(bf16[1024,512]{1,0:T(8,128)(2,1)S(1)} %bitcast.5, bf16[512,1024]{1,0:T(8,128)(2,1)S(1)} %copy-done), kind=kOutput, calls=%fused_computation.13 | convolution fusion | flops 1073741824 | bytes 6291456 | tf_op jit(solution)/shard_map/dot_general | solution.py:31
  33.1 128.3 %all-reduce.3 = bf16[1024,1024]{1,0:T(8,128)(2,1)S(1)} all-reduce(f32[1024,1024]{1,0:T(8,128)} %fusion.12), channel_id=1, replica_groups=mesh['row'=16,'col'=8] {'row'}, use_global_device_ids=true, to_apply=%region_1.0 | all-reduce | flops 1048576 | bytes 6291456 | tf_op jit(solution)/shard_map/psum | solution.py:34
  161.5 0.0 all-gather.2.cloned.1.call-done
  161.5 20.7 %fusion.11 = f32[1024,1792]{1,0:T(8,128)} fusion(bf16[1024,3584]{1,0:T(8,128)(2,1)} %all-gather.2.cloned.1.call-done, bf16[3584,1792]{1,0:T(8,128)(2,1)} %param.5), kind=kOutput, calls=%fused_computation.12 | convolution fusion | flops 13153337344 | bytes 27525120 | tf_op jit(solution)/shard_map/dot_general | solution.py:29
  182.2 85.1 %all-reduce.2 = bf16[1024,1792]{1,0:T(8,128)(2,1)} all-reduce(f32[1024,1792]{1,0:T(8,128)} %fusion.11), channel_id=1, replica_groups=mesh['row'=16,'col'=8] {'col'}, use_global_device_ids=true, to_apply=%region_0.0 | all-reduce | flops 1835008 | bytes 11010048 | tf_op jit(solution)/shard_map/psum | solution.py:30
  267.3 0.0 copy-start.2
  267.3 2.5 fusion.1
  269.8 0.0 copy-done.2
  269.8 1.2 fusion.3
  270.9 4.2 %fusion.5 = f32[1792,1024]{1,0:T(8,128)} fusion(bf16[1024,1792]{1,0:T(8,128)(2,1)S(1)} %copy-done.2, bf16[1024,1024]{1,0:T(8,128)(2,1)S(1)} %all-reduce.3), kind=kOutput, calls=%fused_computation.6 | convolution fusion | flops 939524096 | bytes 8781824 | tf_op jit(solution)/shard_map/dot_general | solution.py:41
  275.1 0.0 copy-start.1
  275.1 7.3 %add_multiply_fusion = f32[1792,1024]{1,0:T(8,128)} fusion(f32[1792,1024]{1,0:T(8,128)S(1)} %fusion.1, f32[1792,1024]{1,0:T(8,128)S(1)} %fusion.3, f32[1792,1024]{1,0:T(8,128)} %fusion.5, bf16[1024,1792]{1,0:T(8,128)(2,1)S(1)} %copy-done.2, bf16[1024,1024]{1,0:T(8,128)(2,1)S(1)} %all-reduce.3), kind=kOutput, calls=%fused_computation | convolution fusion | flops 961544192 | bytes 30801920 | tf_op jit(solution)/shard_map/dot_general | solution.py:41
  282.4 0.0 copy-done.1
Async XLA Ops:
  6.5 23.3 %copy-start = (bf16[512,1024]{1,0:T(8,128)(2,1)S(1)}, bf16[512,1024]{1,0:T(8,128)(2,1)}, u32[]{:S(2)}) copy-start(bf16[512,1024]{1,0:T(8,128)(2,1)} %param.7) | copy-start | bytes 3145732
  6.5 154.9 %all-gather.2.cloned.1.call-start = ((), (), s32[]{:S(2)}) async-start(), calls=%async_computation.1 | async-start | bytes 7798784 | tf_op jit(solution)/shard_map/all_gather | solution.py:28
  267.3 2.5 copy-start.2
  275.1 7.3 %copy-start.1 = (bf16[512,1024]{1,0:T(8,128)(2,1)S(1)}, bf16[512,1024]{1,0:T(8,128)(2,1)}, u32[]{:S(2)}) copy-start(bf16[512,1024]{1,0:T(8,128)(2,1)} %param.7) | copy-start | bytes 3145732
Sparse Core Ops, SparseCore 0:
  9.5 99.1 all-gather.1
where the time goes:
time: 290 us; the launch traced here: 289 us
  blocking collectives  235 us (81%)
  matrix products  39.1 us (13%)
  between operations  13.4 us (5%)
    psum x1, blocking collectives, shards(): rotated_grads = lax.psum(partial_grads, 'row').astype(jnp.bfloat16)  128 us
    psum x1, blocking collectives, shards(): rotated_acts = lax.psum(partial_acts, 'col').astype(jnp.bfloat16)  85.1 us
    all_to_all x1, blocking collectives, sent_to_all(): return lax.all_to_all(copies, axis, split_axis=0, concat_axis=0, tiled=True)  21.6 us
    dot_general x1, matrix products, shards(): jnp.dot(tokens_all, act_basis, preferred_element_type=jnp.float32)  20.7 us
    dot_general x4, matrix products, shards(): lax.dot_general(left, right, (((0,), (0,)), ((), ())), preferred_element_...  15.1 us
  transfers between devices with their start and end apart: 1, of which 0 were waited for; matrix products, arithmetic and copies ran while one was open for 1% of the time, Pallas kernels for 0%

commit v1 on v0

v1 whole, which is shorter than its diff:
```python
import jax
import jax.numpy as jnp
from jax import lax
from jax.experimental import pallas as pl
from jax.experimental.pallas import tpu as pltpu
from jax.sharding import PartitionSpec as P

MESH = pl.DeviceIdType.MESH
BF16, F32 = jnp.bfloat16, jnp.float32
TOKENS, KIN, NIN = 1024, 3584, 1792
KOUT, NOUT = 512, 1024
HALF = NIN // 2
GCOL = NOUT // 2
SEQS, LEN = 4, 256

CHUNKS = (
    ("A00", "A01", "A03", "B00", "B10", "B30"),
    ("A10", "A30", "A02", "B01", "B03", "B20"),
    ("A13", "A33", "A20", "B31", "B33", "B02"),
    ("A11", "A31", "A23", "B11", "B13", "B32"),
    ("A12", "A32", "A21", "A22", "B21", "B23", "B12", "B22"),
)
ROW = {}
for _chunk in CHUNKS:
    for _block in _chunk:
        ROW[_block] = 32 * len(ROW)
BASE = [ROW[chunk[0]] for chunk in CHUNKS]
SIZE = [32 * len(chunk) for chunk in CHUNKS]

RATE = {"x": 1 / 46.6e3, "y": 1 / 46.6e3, "z": 1 / 46.6e3, "d": 1 / 600e3}
DELAY = {"x": 2.2, "y": 2.2, "z": 2.2, "d": 1.0}


def ds(start, size, unit):
    if isinstance(start, int):
        return pl.ds(start, size)
    return pl.ds(pl.multiple_of(start, unit), size)


class Plan:
    def __init__(self):
        self.copies, self.steps = {}, {}
        self.acts()
        self.rotate()
        self.grads()
        self.index = {name: n for n, name in enumerate(self.copies)}

    def copy(self, name, link, nbytes, src, dst):
        self.copies[name] = (link, nbytes, src, dst)

    def step(self, name, rank, waits=(), after=(), cost=0.05, work=None, sends=()):
        self.steps[name] = (rank, tuple(waits), tuple(after), cost, work, tuple(sends))

    def acts(self):
        for half, first, second in (("A", "y", "x"), ("B", "x", "y")):

            def key(u, v, half=half):
                return ROW[half + (f"{v}{u}" if half == "A" else f"{u}{v}")]

            def block(row, low, size):
                return lambda c: c.acts.at[pl.ds(row + low, size), :]

            for r in range(5):
                link = first if r == 0 else second
                u = (0, 0, 3, 1, 2)[r]
                at = (lambda o: key(o, 0)) if r == 0 else (lambda o, u=u: key(u, o))
                for sign, far, low in (("+", 3, 0), ("-", 1, 16)):
                    self.copy(f"{half}d{r}{sign}", link + sign, 32 * KIN * 2, block(at(0), 0, 32), block(at(far), 0, 32))
                    self.copy(f"{half}f{r}{sign}", link + sign, 16 * KIN * 2, block(at(far), low, 16), block(at(2), low, 16))
                    self.step(f"{half}F{r}{sign}", 10 + r, [f"{half}d{r}{sign}"], sends=[f"{half}f{r}{sign}"])
            for r in range(2, 5):
                need = {2: [f"{half}d0+"], 3: [f"{half}d0-"], 4: [f"{half}f0+", f"{half}f0-"]}[r]
                previous = [f"{half}F{r - 2}{s}" for s in "+-"] + [f"{o}F{r - 2}{s}" for s in "+-" for o in "AB"]
                self.step(f"{half}D{r}", 20 + r, need, previous, sends=[f"{half}d{r}+", f"{half}d{r}-"])
        self.step("own", 0, work=lambda c: c.wait_local("acts"), sends=[f"{h}d{r}{s}" for r in (0, 1) for h in "AB" for s in "+-"])

    def ring_sum(self, tag, axis, rank, nbytes, rows, send, recv, add, final, start, sends, gate=()):
        def at(ref, d, h):
            return lambda c: ref(c, rows(c, d, h))

        for name, sign, src, slot in (
            ("a", "+", (2, 1), 0), ("a", "-", (2, 0), 1), ("b", "+", (1, 0), 2),
            ("b", "-", (3, 1), 3), ("c", "+", (1, 1), 4), ("c", "-", (3, 0), 5),
        ):
            self.copy(f"{tag}{name}{sign}", axis + sign, nbytes, at(send, *src), lambda c, slot=slot: recv(c, slot))
        begin = [f"{tag}{n}{s}" for n in "ab" for s in "+-"]
        self.step(f"{tag}S", rank, *start, sends=begin)
        for sign, piece, slot in (("+", (1, 1), 0), ("-", (3, 0), 1)):
            self.step(f"{tag}C{sign}", rank + 1, [f"{tag}a{sign}"], [f"{tag}S"], 0.1,
                      lambda c, piece=piece, slot=slot: add(c, rows(c, *piece), slot), [f"{tag}c{sign}"])
        self.step(f"{tag}E", rank + 2, [f"{tag}{n}{s}" for n in "bc" for s in "+-"], [f"{tag}C+", f"{tag}C-"], 0.2,
                  lambda c: final(c, rows), sends)

    def rotate(self):
        for r in range(5):
            base, size = BASE[r], SIZE[r]
            piece, half = size // 4, size // 8
            offset = base // 8
            need = [f"{h}{n}{s}" for h in "AB" for s in "+-"
                    for n in (("d0",), ("d1", "f0"), ("d2", "f1"), ("d3", "f2"), ("d4", "f3", "f4"))[r]]

            def multiply(c, own, base=base, size=size):
                which = c.k if own else 1 - c.k
                out = c.mine if own else c.other
                if own is False and base == 0:
                    c.wait_local("basis")

                @pl.loop(0, 2)
                def _(n):
                    cols = pl.ds(pl.multiple_of(n * 384, 128), 512)
                    out[pl.ds(base, size), cols] = jnp.dot(
                        c.acts[pl.ds(base, size), :], c.basis[which, :, cols], preferred_element_type=F32)

            cost = 1.8 * size / 192
            before = [] if r == 0 else [f"M{r - 1}m"]
            self.copy(f"{r}core", "d", size * HALF * 4,
                      lambda c, base=base, size=size: c.other.at[pl.ds(base, size), :],
                      lambda c, base=base, size=size: c.partner.at[pl.ds(base, size), :])
            self.step(f"M{r}o", 70 + 2 * r, need, before + ["own"], cost, lambda c, f=multiply: f(c, False), [f"{r}core"])
            self.step(f"M{r}m", 71 + 2 * r, (), [f"M{r}o"], cost, lambda c, f=multiply: f(c, True))

            def rows(c, d, h, base=base, piece=piece, half=half):
                return ds(base + lax.rem(c.z + d, 4) * piece + h * half, half, 8)

            def recv(c, slot, offset=offset, half=half):
                return c.zland.at[slot, pl.ds(offset, half), :]

            def add(c, where, slot, offset=offset, half=half):
                c.mine[where, :] += c.zland[slot, pl.ds(offset, half), :]

            def begin(c, base=base, size=size):
                c.mine[pl.ds(base, size), :] += c.partner[pl.ds(base, size), :]

            def final(c, rows, base=base, piece=piece, half=half, offset=offset):
                parts = []
                for h, one, two in ((0, 2, 5), (1, 3, 4)):
                    parts.append(c.mine[rows(c, 0, h), :] + c.zland[one, pl.ds(offset, half), :] + c.zland[two, pl.ds(offset, half), :])
                whole = jnp.concatenate(parts, axis=0).astype(BF16)
                where = ds(base + c.z * piece, piece, 16)
                for core in range(2):
                    @pl.when(c.k == core)
                    def _(core=core):
                        c.rot[where, pl.ds(core * HALF, HALF)] = whole

            def place(d, low=0, width=HALF, base=base, piece=piece):
                def ref(c):
                    z = lax.rem(c.z + d, 4)
                    return c.rot.at[ds(base + z * piece, piece, 16), pl.ds(pl.multiple_of(c.k * HALF + low, 128), width)]
                return ref

            rank = 40 - 4 * r if False else 40
            nb = piece * HALF * 2
            self.ring_sum(f"{r}z", "z", rank, half * HALF * 4, rows, lambda c, w: c.mine.at[w, :], recv, add, final,
                          ([f"{r}core"], [f"M{r}m"], 0.3, begin), [f"{r}g+", f"{r}g-", f"{r}p0"])
            left = 512 if r % 2 else 384
            self.copy(f"{r}g+", "z+", nb, place(0), place(0))
            self.copy(f"{r}g-", "z-", nb, place(0), place(0))
            self.copy(f"{r}h+", "z+", nb * left // HALF, place(3, 0, left), place(3, 0, left))
            self.copy(f"{r}h-", "z-", nb * (HALF - left) // HALF, place(1, left, HALF - left), place(1, left, HALF - left))
            for n, d in (("p0", 0), ("p1", 1), ("p3", 3), ("p2", 2)):
                self.copy(f"{r}{n}", "d", nb, place(d), place(d))
            self.step(f"{r}H+", 38, [f"{r}g+"], sends=[f"{r}h+", f"{r}p3"])
            self.step(f"{r}H-", 38, [f"{r}g-"], sends=[f"{r}h-", f"{r}p1"])
            self.step(f"{r}L", 39, [f"{r}h+", f"{r}h-"], sends=[f"{r}p2"])

            def store(c, r=r):
                for block in CHUNKS[r]:
                    c.store_acts(block)

            self.step(f"{r}W", 60, [f"{r}p{d}" for d in range(4)], [f"{r}L", f"{r}H+", f"{r}H-"], 0.1, store)

    def grads(self):
        nb = 128 * KOUT * 2

        def shard(d, core, low=0, size=128):
            def ref(c):
                k = c.k if core else 1 - c.k
                return c.grads.at[ds((lax.rem(c.z + d, 4) * 2 + k) * 128 + low, size, 16), :]
            return ref

        self.copy("gz+", "z+", nb, shard(0, 1), shard(0, 1))
        self.copy("gz-", "z-", nb, shard(0, 1), shard(0, 1))
        self.copy("gf+", "z+", nb // 2, shard(3, 1, 0, 64), shard(3, 1, 0, 64))
        self.copy("gf-", "z-", nb // 2, shard(1, 1, 64, 64), shard(1, 1, 64, 64))
        for d in range(4):
            self.copy(f"gp{d}", "d", nb, shard(d, 1), shard(d, 1))
        self.step("G0", 1, after=["own"], work=lambda c: c.wait_local("grads"), sends=["gz+", "gz-", "gp0"])
        self.step("GF+", 2, ["gz+"], ["G0"], sends=["gf+", "gp3"])
        self.step("GF-", 2, ["gz-"], ["G0"], sends=["gf-", "gp1"])
        self.step("GL", 2, ["gf+", "gf-"], ["GF+", "GF-"], sends=["gp2"])

        def multiply(c):
            c.wait_local("gbasis")

            @pl.loop(0, 4)
            def _(n):
                where = pl.ds(pl.multiple_of(n * 256, 256), 256)
                part = jnp.dot(c.grads[where, :], c.gbasis[...], preferred_element_type=F32)
                c.gsum[where, :] = part
                c.gsend[where, :] = part.astype(BF16)

        self.step("GM", 3, [f"gp{d}" for d in range(4)], ["GL"], 2.0, multiply)
        for n, (half, one, two) in enumerate((("A", "x", "y"), ("B", "y", "x"))):
            cols = pl.ds(n * GCOL, GCOL)

            def rows1(c, d, h, one=one):
                return ds(lax.rem(c.pos[one] + d, 4) * 256 + h * 128, 128, 16)

            def add1(c, where, slot, n=n, cols=cols):
                c.gsend[where, cols] = (c.gsum[where, cols] + c.land1[n, slot].astype(F32)).astype(BF16)

            def final1(c, rows, n=n, cols=cols):
                for h, p, q in ((0, 2, 5), (1, 3, 4)):
                    total = c.gsum[rows(c, 0, h), cols] + c.land1[n, p].astype(F32) + c.land1[n, q].astype(F32)
                    c.gsum2[n, pl.ds(h * 128, 128), :] = total
                    c.gsend2[n, pl.ds(h * 128, 128), :] = total.astype(BF16)

            self.ring_sum(f"{half}1", one, 30, 128 * GCOL * 2, rows1, lambda c, w, cols=cols: c.gsend.at[w, cols],
                          lambda c, slot, n=n: c.land1.at[n, slot], add1, final1, ((), ["GM"] + GATE1, 0.05, None), ())

            def rows2(c, d, h, two=two):
                return ds(lax.rem(c.pos[two] + d, 4) * 64 + h * 32, 32, 16)

            def add2(c, where, slot, n=n):
                c.gsend2[n, where, :] = (c.gsum2[n, where, :] + c.land2[n, slot].astype(F32)).astype(BF16)

            def piece(c, d1, d2, one=one, two=two):
                return lax.rem(c.pos[one] + d1, 4) * 256 + lax.rem(c.pos[two] + d2, 4) * 64

            def final2(c, rows, n=n, cols=cols, piece=piece):
                for h, p, q in ((0, 2, 5), (1, 3, 4)):
                    total = c.gsum2[n, rows(c, 0, h), :] + c.land2[n, p].astype(F32) + c.land2[n, q].astype(F32)
                    c.gout[ds(piece(c, 0, 0) + h * 32, 32, 16), cols] = total.astype(BF16)

            def place(d1, d2, low=0, size=64, piece=piece, cols=cols):
                return lambda c: c.gout.at[ds(piece(c, d1, d2) + low, size, 16), cols]

            self.ring_sum(f"{half}2", two, 30, 32 * GCOL * 2, rows2, lambda c, w, n=n: c.gsend2.at[n, w],
                          lambda c, slot, n=n: c.land2.at[n, slot], add2, final2, ((), [f"{half}1E"], 0.05, None),
                          [f"{half}e+", f"{half}e-", f"{half}u0+", f"{half}u0-"])
            nb = 64 * GCOL * 2
            self.copy(f"{half}e+", two + "+", nb, place(0, 0), place(0, 0))
            self.copy(f"{half}e-", two + "-", nb, place(0, 0), place(0, 0))
            self.copy(f"{half}h+", two + "+", nb // 2, place(0, 3, 0, 32), place(0, 3, 0, 32))
            self.copy(f"{half}h-", two + "-", nb // 2, place(0, 1, 32, 32), place(0, 1, 32, 32))
            for j in range(4):
                self.copy(f"{half}u{j}+", one + "+", nb, place(0, j), place(0, j))
                self.copy(f"{half}u{j}-", one + "-", nb, place(0, j), place(0, j))
                self.copy(f"{half}v{j}+", one + "+", nb // 2, place(3, j, 0, 32), place(3, j, 0, 32))
                self.copy(f"{half}v{j}-", one + "-", nb // 2, place(1, j, 32, 32), place(1, j, 32, 32))
                for sign in "+-":
                    self.step(f"{half}V{j}{sign}", 34, [f"{half}u{j}{sign}"], sends=[f"{half}v{j}{sign}"])
            self.step(f"{half}H+", 33, [f"{half}e+"], sends=[f"{half}h+", f"{half}u3+", f"{half}u3-"])
            self.step(f"{half}H-", 33, [f"{half}e-"], sends=[f"{half}h-", f"{half}u1+", f"{half}u1-"])
            self.step(f"{half}L", 33, [f"{half}h+", f"{half}h-"], sends=[f"{half}u2+", f"{half}u2-"])
        every = [f"{h}v{j}{s}" for h in "AB" for j in range(4) for s in "+-"]
        self.step("GW", 80, every, cost=0.1, work=lambda c: c.store_grads())

    def order(self, trace=None):
        now, arrival, free, done, todo, order = 0.0, {}, {}, {}, dict(self.steps), []
        sent_by = {name for spec in self.steps.values() for name in spec[5]}
        assert sent_by == set(self.copies)
        while todo:
            best, soonest = None, None
            for name, (rank, waits, after, cost, _, sends) in todo.items():
                if any(a not in done for a in after) or any(w not in arrival for w in waits):
                    continue
                at = max([arrival[w] for w in waits], default=0.0)
                if at <= now and (best is None or rank < best[0]):
                    best = (rank, name)
                if soonest is None or at < soonest:
                    soonest = at
            if best is None:
                assert soonest is not None, sorted(todo)
                now = soonest
                continue
            name = best[1]
            rank, waits, after, cost, _, sends = todo.pop(name)
            now += cost
            done[name] = now
            order.append(name)
            if trace is not None:
                trace.append((now, name))
            for copy in sends:
                link, nbytes = self.copies[copy][:2]
                free[link] = max(now, free.get(link, 0.0)) + nbytes * RATE[link[0]]
                arrival[copy] = free[link] + DELAY[link[0]]
                if trace is not None:
                    trace.append((arrival[copy], "  arrives " + copy + " " + link))
        return order


GATE1 = ["AD4", "BD4"]


class Context:
    pass


def rotate_kernel(plan, acts_in, basis_in, grads_in, gbasis_in, rot_out, grad_out,
                  acts, basis, mine, other, partner, zland, rot, grads, gbasis, gsum, gsend, gsum2, gsend2, land1, land2, gout,
                  send_sem, recv_sem, load_sem, store_sem):
    c = Context()
    c.acts, c.basis, c.mine, c.other, c.partner, c.zland, c.rot = acts, basis, mine, other, partner, zland, rot
    c.grads, c.gbasis, c.gsum, c.gsend, c.gsum2, c.gsend2 = grads, gbasis, gsum, gsend, gsum2, gsend2
    c.land1, c.land2, c.gout = land1, land2, gout
    row, col = lax.axis_index("row"), lax.axis_index("col")
    c.pos = {"x": row // 4, "y": lax.rem(row, 4)}
    c.z, c.k = col // 2, lax.rem(col, 2)

    def peer(link):
        if link == "d":
            return (row, c.z * 2 + 1 - c.k)
        step = 1 if link[1] == "+" else 3
        if link[0] == "z":
            return (row, lax.rem(c.z + step, 4) * 2 + c.k)
        if link[0] == "x":
            return (lax.rem(c.pos["x"] + step, 4) * 4 + c.pos["y"], col)
        return (c.pos["x"] * 4 + lax.rem(c.pos["y"] + step, 4), col)

    me = col * 128
    loads = {
        "acts": [(acts_in.at[pl.ds(0, 32), :], acts.at[pl.ds(ROW["A00"], 32), :]),
                 (acts_in.at[pl.ds(32, 32), :], acts.at[pl.ds(ROW["B00"], 32), :])],
        "grads": [(grads_in, grads.at[ds(me, 128, 128), :])],
        "gbasis": [(gbasis_in, gbasis)],
        "basis": [(basis_in.at[pl.ds(q * 896, 896), pl.ds(h * HALF, HALF)], basis.at[h, pl.ds(q * 896, 896), :])
                  for q in range(4) for h in range(2)],
    }
    number, local = 0, {}
    for name, pairs in loads.items():
        local[name] = []
        for src, dst in pairs:
            local[name].append(pltpu.make_async_copy(src, dst, load_sem.at[number]))
            number += 1
            local[name][-1].start()

    def wait_local(name):
        for one in local[name]:
            one.wait()

    c.wait_local = wait_local
    stores = []

    def store(src, dst):
        stores.append(pltpu.make_async_copy(src, dst, store_sem.at[len(stores)]))
        stores[-1].start()

    def store_acts(block):
        x, y = lax.rem(c.pos["x"] + int(block[1]), 4), lax.rem(c.pos["y"] + int(block[2]), 4)
        to = (x * 4 + y) * 64 + (0 if block[0] == "A" else 32)
        store(rot.at[pl.ds(ROW[block], 32), :], rot_out.at[ds(to, 32, 32), :])

    c.store_acts = store_acts
    c.store_grads = lambda: store(gout, grad_out)

    barrier = pltpu.get_barrier_semaphore()
    links = ("x+", "x-", "y+", "y-", "z+", "z-", "d")
    for link in links:
        pl.semaphore_signal(barrier, inc=1, device_id=peer(link), device_id_type=MESH)
    pl.semaphore_wait(barrier, len(links))

    started = {}

    def copy_of(name):
        link, _, src, dst = plan.copies[name]
        n = plan.index[name]
        return pltpu.make_async_remote_copy(src_ref=src(c), dst_ref=dst(c), send_sem=send_sem.at[n], recv_sem=recv_sem.at[n],
                                            device_id=peer(link), device_id_type=MESH)

    waited = set()
    for name in plan.order():
        _, waits, _, _, work, sends = plan.steps[name]
        for one in waits:
            if one not in waited:
                waited.add(one)
                started[one].wait_recv()
        if work is not None:
            work(c)
        for one in sends:
            started[one] = copy_of(one)
            started[one].start()
    assert waited == set(plan.copies)
    for one in started.values():
        one.wait_send()
    for one in stores:
        one.wait()


def rotate(activations, act_basis, grads, grad_basis):
    plan = Plan()
    count = len(plan.copies)
    anywhere = pl.BlockSpec(memory_space=pl.ANY)
    return pl.pallas_call(
        lambda *refs: rotate_kernel(plan, *refs),
        out_shape=[jax.ShapeDtypeStruct((TOKENS, NIN), BF16), jax.ShapeDtypeStruct((TOKENS, NOUT), BF16)],
        in_specs=[anywhere] * 4,
        out_specs=[anywhere] * 2,
        scratch_shapes=[
            pltpu.VMEM((TOKENS, KIN), BF16),
            pltpu.VMEM((2, KIN, HALF), BF16),
            pltpu.VMEM((TOKENS, HALF), F32),
            pltpu.VMEM((TOKENS, HALF), F32),
            pltpu.VMEM((TOKENS, HALF), F32),
            pltpu.VMEM((6, TOKENS // 8, HALF), F32),
            pltpu.VMEM((TOKENS, NIN), BF16),
            pltpu.VMEM((TOKENS, KOUT), BF16),
            pltpu.VMEM((KOUT, NOUT), BF16),
            pltpu.VMEM((TOKENS, NOUT), F32),
            pltpu.VMEM((TOKENS, NOUT), BF16),
            pltpu.VMEM((2, 256, GCOL), F32),
            pltpu.VMEM((2, 256, GCOL), BF16),
            pltpu.VMEM((2, 6, 128, GCOL), BF16),
            pltpu.VMEM((2, 6, 32, GCOL), BF16),
            pltpu.VMEM((TOKENS, NOUT), BF16),
            pltpu.SemaphoreType.DMA((count,)),
            pltpu.SemaphoreType.DMA((count,)),
            pltpu.SemaphoreType.DMA((12,)),
            pltpu.SemaphoreType.DMA((33,)),
        ],
        compiler_params=pltpu.CompilerParams(collective_id=0, has_side_effects=True, vmem_limit_bytes=60 * 2**20),
        name="rotate",
    )(activations, act_basis, grads, grad_basis)


def square_kernel(rot, grad, out):
    total = None
    for s in range(SEQS):
        where = pl.ds(s * LEN, LEN)
        products = lax.dot_general(rot[where, :], grad[where, :], (((0,), (0,)), ((), ())), preferred_element_type=F32)
        total = products * products if total is None else total + products * products
    out[...] = total * (1.0 / (LEN * SEQS))


def square(rot, grad):
    rows = 256
    return pl.pallas_call(
        square_kernel,
        out_shape=jax.ShapeDtypeStruct((NIN, NOUT), F32),
        grid=(NIN // rows,),
        in_specs=[pl.BlockSpec((TOKENS, rows), lambda i: (0, i)), pl.BlockSpec((TOKENS, NOUT), lambda i: (0, 0))],
        out_specs=pl.BlockSpec((rows, NOUT), lambda i: (i, 0)),
        compiler_params=pltpu.CompilerParams(dimension_semantics=("arbitrary",)),
        name="square",
    )(rot, grad)


def shards(activations, act_basis, grads, grad_basis):
    return square(*rotate(activations, act_basis, grads, grad_basis))


def solution(mesh):
    return jax.shard_map(
        shards,
        mesh=mesh,
        in_specs=(P("row", "col"), P("col", "row"), P("col", "row"), P("row", "col")),
        out_specs=P("row", "col"),
        check_vma=False,
    )
```

time: 290 us -> 96.2 us (0.33)
  blocking collectives: 235 us -> 0 us
  Pallas kernels: 0 us -> 95.7 us
  matrix products: 39.1 us -> 0 us
  between operations: 13.4 us -> 0.01 us
    psum x2 -> x0, blocking collectives: 213 us -> none  [the longest x1 128 us: shards(): rotated_grads = lax.psum(partial_grads, 'row').astype(jnp.bfloat16)]
    pallas_call x0 -> x2, Pallas kernels: none -> 95.7 us  [the longest x1 85.6 us: rotate(): pl.pallas_call(lambda *refs: rotate_kernel(plan, *refs), out_shape=[jax.S...]
    dot_general x6 -> x0, matrix products: 39.1 us -> none  [the longest x1 20.7 us: shards(): jnp.dot(tokens_all, act_basis, preferred_element_type=jnp.float32)]
    all_to_all x1 -> x0, blocking collectives: 21.6 us -> none  [sent_to_all(): return lax.all_to_all(copies, axis, split_axis=0, concat_axis=0, tiled=True)]
  transfers between devices with their start and end apart: 1 -> 0, of which waited for: 0 -> 0; matrix products, arithmetic and copies ran while one was open for 1% -> 0% of each run, Pallas kernels for 0% -> 0%
where the time goes in v1:
time: 96.2 us; the launch traced here: 95.7 us
  Pallas kernels  95.7 us (99%)
    pallas_call x1, Pallas kernels, rotate(): pl.pallas_call(lambda *refs: rotate_kernel(plan, *refs), out_shape=[jax.S...  85.6 us
    pallas_call x1, Pallas kernels, square(): pl.pallas_call(square_kernel, out_shape=jax.ShapeDtypeStruct((NIN, NOUT),...  10.1 us

profile of v1, /device:TPU:1, one launch (start us, length us, event | category | flops | bytes accessed | tf_op | source)
XLA Modules:
  0.0 95.7 jit_solution(3089851938735318462)
XLA Ops:
  0.0 85.6 %rotate.1 = (bf16[1024,1792]{1,0:T(8,128)(2,1)}, bf16[1024,1024]{1,0:T(8,128)(2,1)}) custom-call(bf16[64,3584]{1,0:T(8,128)(2,1)} %refs_0_.1, bf16[3584,1792]{1,0:T(8,128)(2,1)} %refs_1_.1, bf16[128,512]{1,0:T(8,128)(2,1)} %refs_2_.1, bf16[512,1024]{1,0:T(8,128)(2,1)} %refs_3_.1), custom_call_target="tpu_custom_call" | custom-call | tf_op jit(solution)/shard_map/rotate/pallas_call | solution.py:394
  85.6 10.1 %square.1 = f32[1792,1024]{1,0:T(8,128)} custom-call(bf16[1024,1792]{1,0:T(8,128)(2,1)} %get-tuple-element.7.rot, bf16[1024,1024]{1,0:T(8,128)(2,1)} %get-tuple-element.8.grad), custom_call_target="tpu_custom_call" | custom-call | tf_op jit(solution)/shard_map/square/pallas_call | solution.py:437

commit v2 on v1

--- a/solution.py
+++ b/solution.py
@@ -12,13 +12,15 @@
 HALF = NIN // 2
 GCOL = NOUT // 2
 SEQS, LEN = 4, 256
+PARTS = ((0, 512), (512, 384))
 
 CHUNKS = (
     ("A00", "A01", "A03", "B00", "B10", "B30"),
     ("A10", "A30", "A02", "B01", "B03", "B20"),
     ("A13", "A33", "A20", "B31", "B33", "B02"),
     ("A11", "A31", "A23", "B11", "B13", "B32"),
-    ("A12", "A32", "A21", "A22", "B21", "B23", "B12", "B22"),
+    ("A12", "A32", "A21", "B21", "B23", "B12"),
+    ("A22", "B22"),
 )
 ROW = {}
 for _chunk in CHUNKS:
@@ -26,9 +28,6 @@
         ROW[_block] = 32 * len(ROW)
 BASE = [ROW[chunk[0]] for chunk in CHUNKS]
 SIZE = [32 * len(chunk) for chunk in CHUNKS]
-
-RATE = {"x": 1 / 46.6e3, "y": 1 / 46.6e3, "z": 1 / 46.6e3, "d": 1 / 600e3}
-DELAY = {"x": 2.2, "y": 2.2, "z": 2.2, "d": 1.0}
 
 
 def ds(start, size, unit):
@@ -92,32 +91,35 @@
                   lambda c: final(c, rows), sends)
 
     def rotate(self):
-        for r in range(5):
+        for r in range(6):
             base, size = BASE[r], SIZE[r]
             piece, half = size // 4, size // 8
             offset = base // 8
             need = [f"{h}{n}{s}" for h in "AB" for s in "+-"
-                    for n in (("d0",), ("d1", "f0"), ("d2", "f1"), ("d3", "f2"), ("d4", "f3", "f4"))[r]]
-
-            def multiply(c, own, base=base, size=size):
+                    for n in (("d0",), ("d1", "f0"), ("d2", "f1"), ("d3", "f2"), ("d4", "f3"), ("f4",))[r]]
+
+            def multiply(c, own, cols, base=base, size=size):
                 which = c.k if own else 1 - c.k
                 out = c.mine if own else c.other
-                if own is False and base == 0:
+                if not own and base == 0 and cols == PARTS[0]:
                     c.wait_local("basis")
-
-                @pl.loop(0, 2)
-                def _(n):
-                    cols = pl.ds(pl.multiple_of(n * 384, 128), 512)
-                    out[pl.ds(base, size), cols] = jnp.dot(
-                        c.acts[pl.ds(base, size), :], c.basis[which, :, cols], preferred_element_type=F32)
-
-            cost = 1.8 * size / 192
-            before = [] if r == 0 else [f"M{r - 1}m"]
-            self.copy(f"{r}core", "d", size * HALF * 4,
-                      lambda c, base=base, size=size: c.other.at[pl.ds(base, size), :],
-                      lambda c, base=base, size=size: c.partner.at[pl.ds(base, size), :])
-            self.step(f"M{r}o", 70 + 2 * r, need, before + ["own"], cost, lambda c, f=multiply: f(c, False), [f"{r}core"])
-            self.step(f"M{r}m", 71 + 2 * r, (), [f"M{r}o"], cost, lambda c, f=multiply: f(c, True))
+                where, cols = pl.ds(base, size), pl.ds(*cols)
+                out[where, cols] = jnp.dot(c.acts[where, :], c.basis[which, :, cols], preferred_element_type=F32)
+
+            cost = {192: 0.88, 64: 0.62}[size]
+            last = f"M{r - 1}m1" if r else "own"
+            for own in (False, True):
+                for n, cols in enumerate(PARTS):
+                    name = f"M{r}{'m' if own else 'o'}{n}"
+                    sends = []
+                    if not own:
+                        sends = [f"{r}core{n}"]
+                        self.copy(sends[0], "d", size * cols[1] * 4,
+                                  lambda c, base=base, size=size, cols=cols: c.other.at[pl.ds(base, size), pl.ds(*cols)],
+                                  lambda c, base=base, size=size, cols=cols: c.partner.at[pl.ds(base, size), pl.ds(*cols)])
+                    self.step(name, 70 + 4 * r + 2 * own + n, () if own or n else need, [last], cost,
+                              lambda c, f=multiply, own=own, cols=cols: f(c, own, cols), sends)
+                    last = name
 
             def rows(c, d, h, base=base, piece=piece, half=half):
                 return ds(base + lax.rem(c.z + d, 4) * piece + h * half, half, 8)
@@ -148,10 +150,10 @@
                     return c.rot.at[ds(base + z * piece, piece, 16), pl.ds(pl.multiple_of(c.k * HALF + low, 128), width)]
                 return ref
 
-            rank = 40 - 4 * r if False else 40
+            rank = 40
             nb = piece * HALF * 2
             self.ring_sum(f"{r}z", "z", rank, half * HALF * 4, rows, lambda c, w: c.mine.at[w, :], recv, add, final,
-                          ([f"{r}core"], [f"M{r}m"], 0.3, begin), [f"{r}g+", f"{r}g-", f"{r}p0"])
+                          ([f"{r}core0", f"{r}core1"], [f"M{r}m1"], 0.3, begin), [f"{r}g+", f"{r}g-", f"{r}p0"])
             left = 512 if r % 2 else 384
             self.copy(f"{r}g+", "z+", nb, place(0), place(0))
             self.copy(f"{r}g-", "z-", nb, place(0), place(0))
@@ -163,11 +165,7 @@
             self.step(f"{r}H-", 38, [f"{r}g-"], sends=[f"{r}h-", f"{r}p1"])
             self.step(f"{r}L", 39, [f"{r}h+", f"{r}h-"], sends=[f"{r}p2"])
 
-            def store(c, r=r):
-                for block in CHUNKS[r]:
-                    c.store_acts(block)
-
-            self.step(f"{r}W", 60, [f"{r}p{d}" for d in range(4)], [f"{r}L", f"{r}H+", f"{r}H-"], 0.1, store)
+            self.step(f"{r}W", 90, [f"{r}p{d}" for d in range(4)], [f"{r}L", f"{r}H+", f"{r}H-"])
 
     def grads(self):
         nb = 128 * KOUT * 2
@@ -216,7 +214,7 @@
                     c.gsend2[n, pl.ds(h * 128, 128), :] = total.astype(BF16)
 
             self.ring_sum(f"{half}1", one, 30, 128 * GCOL * 2, rows1, lambda c, w, cols=cols: c.gsend.at[w, cols],
-                          lambda c, slot, n=n: c.land1.at[n, slot], add1, final1, ((), ["GM"] + GATE1, 0.05, None), ())
+                          lambda c, slot, n=n: c.land1.at[n, slot], add1, final1, ((), ["GM"], 0.05, None), ())
 
             def rows2(c, d, h, two=two):
                 return ds(lax.rem(c.pos[two] + d, 4) * 64 + h * 32, 32, 16)
@@ -254,52 +252,29 @@
             self.step(f"{half}H-", 33, [f"{half}e-"], sends=[f"{half}h-", f"{half}u1+", f"{half}u1-"])
             self.step(f"{half}L", 33, [f"{half}h+", f"{half}h-"], sends=[f"{half}u2+", f"{half}u2-"])
         every = [f"{h}v{j}{s}" for h in "AB" for j in range(4) for s in "+-"]
-        self.step("GW", 80, every, cost=0.1, work=lambda c: c.store_grads())
-
-    def order(self, trace=None):
-        now, arrival, free, done, todo, order = 0.0, {}, {}, {}, dict(self.steps), []
-        sent_by = {name for spec in self.steps.values() for name in spec[5]}
-        assert sent_by == set(self.copies)
-        while todo:
-            best, soonest = None, None
-            for name, (rank, waits, after, cost, _, sends) in todo.items():
-                if any(a not in done for a in after) or any(w not in arrival for w in waits):
-                    continue
-                at = max([arrival[w] for w in waits], default=0.0)
-                if at <= now and (best is None or rank < best[0]):
-                    best = (rank, name)
-                if soonest is None or at < soonest:
-                    soonest = at
-            if best is None:
-                assert soonest is not None, sorted(todo)
-                now = soonest
-                continue
-            name = best[1]
-            rank, waits, after, cost, _, sends = todo.pop(name)
-            now += cost
-            done[name] = now
-            order.append(name)
-            if trace is not None:
-                trace.append((now, name))
-            for copy in sends:
-                link, nbytes = self.copies[copy][:2]
-                free[link] = max(now, free.get(link, 0.0)) + nbytes * RATE[link[0]]
-                arrival[copy] = free[link] + DELAY[link[0]]
-                if trace is not None:
-                    trace.append((arrival[copy], "  arrives " + copy + " " + link))
-        return order
-
-
-GATE1 = ["AD4", "BD4"]
+        self.step("GW", 90, every)
+
+
+ORDER = (
+    "own", "G0", "M0o0", "AF0+", "M0o1", "GF-", "BF0-", "AF0-", "BF0+", "AD2", "BD2", "GF+", "BF1-", "M0m0", "AF1+", "M0m1",
+    "M1o0", "0zS", "AF1-", "BF1+", "M1o1", "M1m0", "AD3", "GL", "M1m1", "BD3", "1zS", "GM", "0zC-", "AF2+", "AF2-", "BF2+",
+    "M2o0", "0zC+", "BF2-", "M2o1", "M2m0", "A1S", "1zC-", "AD4", "B1S", "1zC+", "M2m1", "BD4", "2zS", "0zE", "M3o0", "M3o1",
+    "M3m0", "2zC+", "2zC-", "M3m1", "A1C-", "A1C+", "3zS", "B1C+", "B1C-", "1zE", "3zC+", "3zC-", "AF3+", "BF3-", "BF3+",
+    "AF3-", "1H-", "B1E", "BF4+", "0H-", "B2S", "BF4-", "2zE", "A1E", "0H+", "AF4+", "AF4-", "A2S", "3zE", "1H+", "M4o0",
+    "M4o1", "B2C+", "B2C-", "M4m0", "M4m1", "4zS", "A2C+", "A2C-", "M5o0", "B2E", "M5o1", "M5m0", "M5m1", "0L", "5zS", "A2E",
+    "4zC+", "4zC-", "BH-", "BH+", "5zC-", "2H-", "5zC+", "AH+", "2H+", "AH-", "BL", "4zE", "5zE", "BV1-", "3H+", "BV1+",
+    "1L", "AV0-", "BV0-", "3H-", "AL", "BV0+", "BV3+", "AV0+", "0W", "AV3-", "BV3-", "BV2-", "BV2+", "AV1+", "AV3+", "AV1-",
+    "4H-", "4H+", "5H+", "5H-", "AV2+", "AV2-", "3L", "2L", "3W", "4L", "2W", "5L", "1W", "4W", "GW", "5W",
+)
 
 
 class Context:
     pass
 
 
-def rotate_kernel(plan, acts_in, basis_in, grads_in, gbasis_in, rot_out, grad_out,
-                  acts, basis, mine, other, partner, zland, rot, grads, gbasis, gsum, gsend, gsum2, gsend2, land1, land2, gout,
-                  send_sem, recv_sem, load_sem, store_sem):
+def rotate_kernel(plan, acts_in, basis_in, grads_in, gbasis_in, rot, gout,
+                  acts, basis, mine, other, partner, zland, grads, gbasis, gsum, gsend, gsum2, gsend2, land1, land2,
+                  send_sem, recv_sem, load_sem):
     c = Context()
     c.acts, c.basis, c.mine, c.other, c.partner, c.zland, c.rot = acts, basis, mine, other, partner, zland, rot
     c.grads, c.gbasis, c.gsum, c.gsend, c.gsum2, c.gsend2 = grads, gbasis, gsum, gsend, gsum2, gsend2
@@ -340,20 +315,6 @@
             one.wait()
 
     c.wait_local = wait_local
-    stores = []
-
-    def store(src, dst):
-        stores.append(pltpu.make_async_copy(src, dst, store_sem.at[len(stores)]))
-        stores[-1].start()
-
-    def store_acts(block):
-        x, y = lax.rem(c.pos["x"] + int(block[1]), 4), lax.rem(c.pos["y"] + int(block[2]), 4)
-        to = (x * 4 + y) * 64 + (0 if block[0] == "A" else 32)
-        store(rot.at[pl.ds(ROW[block], 32), :], rot_out.at[ds(to, 32, 32), :])
-
-    c.store_acts = store_acts
-    c.store_grads = lambda: store(gout, grad_out)
-
     barrier = pltpu.get_barrier_semaphore()
     links = ("x+", "x-", "y+", "y-", "z+", "z-", "d")
     for link in links:
@@ -369,7 +330,7 @@
                                             device_id=peer(link), device_id_type=MESH)
 
     waited = set()
-    for name in plan.order():
+    for name in ORDER:
         _, waits, _, _, work, sends = plan.steps[name]
         for one in waits:
             if one not in waited:
@@ -383,8 +344,6 @@
     assert waited == set(plan.copies)
     for one in started.values():
         one.wait_send()
-    for one in stores:
-        one.wait()
 
 
 def rotate(activations, act_basis, grads, grad_basis):
@@ -393,9 +352,9 @@
     anywhere = pl.BlockSpec(memory_space=pl.ANY)
     return pl.pallas_call(
         lambda *refs: rotate_kernel(plan, *refs),
-        out_shape=[jax.ShapeDtypeStruct((TOKENS, NIN), BF16), jax.ShapeDtypeStruct((TOKENS, NOUT), BF16)],
+        out_shape=[pltpu.VMEM((TOKENS, NIN), BF16), pltpu.VMEM((TOKENS, NOUT), BF16)],
         in_specs=[anywhere] * 4,
-        out_specs=[anywhere] * 2,
+        out_specs=[pl.BlockSpec(memory_space=pltpu.VMEM)] * 2,
         scratch_shapes=[
             pltpu.VMEM((TOKENS, KIN), BF16),
             pltpu.VMEM((2, KIN, HALF), BF16),
@@ -403,7 +362,6 @@
             pltpu.VMEM((TOKENS, HALF), F32),
             pltpu.VMEM((TOKENS, HALF), F32),
             pltpu.VMEM((6, TOKENS // 8, HALF), F32),
-            pltpu.VMEM((TOKENS, NIN), BF16),
             pltpu.VMEM((TOKENS, KOUT), BF16),
             pltpu.VMEM((KOUT, NOUT), BF16),
             pltpu.VMEM((TOKENS, NOUT), F32),
@@ -412,22 +370,28 @@
             pltpu.VMEM((2, 256, GCOL), BF16),
             pltpu.VMEM((2, 6, 128, GCOL), BF16),
             pltpu.VMEM((2, 6, 32, GCOL), BF16),
-            pltpu.VMEM((TOKENS, NOUT), BF16),
             pltpu.SemaphoreType.DMA((count,)),
             pltpu.SemaphoreType.DMA((count,)),
             pltpu.SemaphoreType.DMA((12,)),
-            pltpu.SemaphoreType.DMA((33,)),
         ],
-        compiler_params=pltpu.CompilerParams(collective_id=0, has_side_effects=True, vmem_limit_bytes=60 * 2**20),
+        compiler_params=pltpu.CompilerParams(collective_id=0, has_side_effects=True, vmem_limit_bytes=50 * 2**20),
         name="rotate",
     )(activations, act_basis, grads, grad_basis)
 
 
 def square_kernel(rot, grad, out):
+    row = lax.axis_index("row")
+    x, y = row // 4, lax.rem(row, 4)
     total = None
-    for s in range(SEQS):
-        where = pl.ds(s * LEN, LEN)
-        products = lax.dot_general(rot[where, :], grad[where, :], (((0,), (0,)), ((), ())), preferred_element_type=F32)
+    for i in range(4):
+        blocks = [(half, i, j) for half in "AB" for j in range(4)]
+        left = jnp.concatenate([rot[pl.ds(ROW[f"{h}{i}{j}"], 32), :] for h, i, j in blocks], axis=0)
+        right = []
+        for h, i, j in blocks:
+            token = (lax.rem(x + i, 4) * 4 + lax.rem(y + j, 4)) * 64 + (0 if h == "A" else 32)
+            right.append(grad[ds(token, 32, 32), :])
+        right = jnp.concatenate(right, axis=0)
+        products = lax.dot_general(left, right, (((0,), (0,)), ((), ())), preferred_element_type=F32)
         total = products * products if total is None else total + products * products
     out[...] = total * (1.0 / (LEN * SEQS))
 
@@ -440,7 +404,7 @@
         grid=(NIN // rows,),
         in_specs=[pl.BlockSpec((TOKENS, rows), lambda i: (0, i)), pl.BlockSpec((TOKENS, NOUT), lambda i: (0, 0))],
         out_specs=pl.BlockSpec((rows, NOUT), lambda i: (i, 0)),
-        compiler_params=pltpu.CompilerParams(dimension_semantics=("arbitrary",)),
+        compiler_params=pltpu.CompilerParams(dimension_semantics=("arbitrary",), vmem_limit_bytes=20 * 2**20),
         name="square",
     )(rot, grad)
 

time: 96.2 us -> 87.1 us (0.905)
  Pallas kernels: 95.7 us -> 86.9 us
    pallas_call x1, Pallas kernels: 85.6 us -> 79.9 us  [rotate(): pl.pallas_call(lambda *refs: rotate_kernel(plan, *refs), out_shape=[pltpu...]
    pallas_call x1, Pallas kernels: 10.1 us -> 7.06 us  [square(): pl.pallas_call(square_kernel, out_shape=jax.ShapeDtypeStruct((NIN, NOUT),...]
where the time goes in v2:
time: 87.1 us; the launch traced here: 87 us
  Pallas kernels  86.9 us (100%)
    pallas_call x1, Pallas kernels, rotate(): pl.pallas_call(lambda *refs: rotate_kernel(plan, *refs), out_shape=[pltpu...  79.9 us
    pallas_call x1, Pallas kernels, square(): pl.pallas_call(square_kernel, out_shape=jax.ShapeDtypeStruct((NIN, NOUT),...  7.06 us

profile of v2, /device:TPU:1, one launch (start us, length us, event | category | flops | bytes accessed | tf_op | source)
XLA Modules:
  0.0 87.0 jit_solution(1236881956023533722)
XLA Ops:
  0.0 79.9 %rotate.1 = (bf16[1024,1792]{1,0:T(8,128)(2,1)S(1)}, bf16[1024,1024]{1,0:T(8,128)(2,1)S(1)}) custom-call(bf16[64,3584]{1,0:T(8,128)(2,1)} %refs_0_.1, bf16[3584,1792]{1,0:T(8,128)(2,1)} %refs_1_.1, bf16[128,512]{1,0:T(8,128)(2,1)} %refs_2_.1, bf16[512,1024]{1,0:T(8,128)(2,1)} %refs_3_.1), custom_call_target="tpu_custom_call" | custom-call | tf_op jit(solution)/shard_map/rotate/pallas_call | solution.py:353
  79.9 7.1 %square.1 = f32[1792,1024]{1,0:T(8,128)} custom-call(bf16[1024,1792]{1,0:T(8,128)(2,1)S(1)} %get-tuple-element.7.rot, bf16[1024,1024]{1,0:T(8,128)(2,1)S(1)} %get-tuple-element.8.grad), custom_call_target="tpu_custom_call" | custom-call | tf_op jit(solution)/shard_map/square/pallas_call | solution.py:401

commit v3 on v2

--- a/solution.py
+++ b/solution.py
@@ -10,7 +10,7 @@
 TOKENS, KIN, NIN = 1024, 3584, 1792
 KOUT, NOUT = 512, 1024
 HALF = NIN // 2
-GCOL = NOUT // 2
+GCOL = NOUT // 4
 SEQS, LEN = 4, 256
 PARTS = ((0, 512), (512, 384))
 
@@ -29,7 +29,6 @@
 BASE = [ROW[chunk[0]] for chunk in CHUNKS]
 SIZE = [32 * len(chunk) for chunk in CHUNKS]
 
-
 def ds(start, size, unit):
     if isinstance(start, int):
         return pl.ds(start, size)
@@ -198,7 +197,7 @@
                 c.gsend[where, :] = part.astype(BF16)
 
         self.step("GM", 3, [f"gp{d}" for d in range(4)], ["GL"], 2.0, multiply)
-        for n, (half, one, two) in enumerate((("A", "x", "y"), ("B", "y", "x"))):
+        for n, (half, one, two) in enumerate((("A", "x", "y"), ("B", "y", "x"), ("C", "x", "y"), ("D", "y", "x"))):
             cols = pl.ds(n * GCOL, GCOL)
 
             def rows1(c, d, h, one=one):
@@ -251,20 +250,18 @@
             self.step(f"{half}H+", 33, [f"{half}e+"], sends=[f"{half}h+", f"{half}u3+", f"{half}u3-"])
             self.step(f"{half}H-", 33, [f"{half}e-"], sends=[f"{half}h-", f"{half}u1+", f"{half}u1-"])
             self.step(f"{half}L", 33, [f"{half}h+", f"{half}h-"], sends=[f"{half}u2+", f"{half}u2-"])
-        every = [f"{h}v{j}{s}" for h in "AB" for j in range(4) for s in "+-"]
+        every = [f"{h}v{j}{s}" for h in "ABCD" for j in range(4) for s in "+-"]
         self.step("GW", 90, every)
 
 
 ORDER = (
-    "own", "G0", "M0o0", "AF0+", "M0o1", "GF-", "BF0-", "AF0-", "BF0+", "AD2", "BD2", "GF+", "BF1-", "M0m0", "AF1+", "M0m1",
-    "M1o0", "0zS", "AF1-", "BF1+", "M1o1", "M1m0", "AD3", "GL", "M1m1", "BD3", "1zS", "GM", "0zC-", "AF2+", "AF2-", "BF2+",
-    "M2o0", "0zC+", "BF2-", "M2o1", "M2m0", "A1S", "1zC-", "AD4", "B1S", "1zC+", "M2m1", "BD4", "2zS", "0zE", "M3o0", "M3o1",
-    "M3m0", "2zC+", "2zC-", "M3m1", "A1C-", "A1C+", "3zS", "B1C+", "B1C-", "1zE", "3zC+", "3zC-", "AF3+", "BF3-", "BF3+",
-    "AF3-", "1H-", "B1E", "BF4+", "0H-", "B2S", "BF4-", "2zE", "A1E", "0H+", "AF4+", "AF4-", "A2S", "3zE", "1H+", "M4o0",
-    "M4o1", "B2C+", "B2C-", "M4m0", "M4m1", "4zS", "A2C+", "A2C-", "M5o0", "B2E", "M5o1", "M5m0", "M5m1", "0L", "5zS", "A2E",
-    "4zC+", "4zC-", "BH-", "BH+", "5zC-", "2H-", "5zC+", "AH+", "2H+", "AH-", "BL", "4zE", "5zE", "BV1-", "3H+", "BV1+",
-    "1L", "AV0-", "BV0-", "3H-", "AL", "BV0+", "BV3+", "AV0+", "0W", "AV3-", "BV3-", "BV2-", "BV2+", "AV1+", "AV3+", "AV1-",
-    "4H-", "4H+", "5H+", "5H-", "AV2+", "AV2-", "3L", "2L", "3W", "4L", "2W", "5L", "1W", "4W", "GW", "5W",
+    26, 99, 13, 1, 14, 101, 0, 23, 100, 27, 10, 28, 29, 15, 2, 3, 30, 102, 16, 31, 39, 103, 123, 40, 104, 41, 17, 42, 43, 24,
+    11, 51, 32, 18, 5, 52, 106, 4, 33, 105, 53, 54, 45, 125, 44, 55, 12, 124, 161, 142, 25, 46, 63, 34, 57, 56, 64, 7, 65,
+    20, 126, 66, 19, 67, 6, 143, 162, 163, 127, 144, 9, 48, 21, 47, 107, 22, 58, 108, 36, 68, 8, 35, 69, 75, 76, 164, 165,
+    128, 145, 146, 129, 77, 78, 79, 110, 109, 87, 166, 167, 88, 148, 147, 130, 89, 90, 91, 111, 168, 80, 81, 149, 139, 140,
+    70, 93, 120, 121, 177, 178, 92, 158, 159, 82, 169, 122, 170, 141, 137, 94, 179, 160, 71, 60, 115, 172, 59, 132, 153, 138,
+    118, 175, 150, 72, 119, 37, 112, 131, 114, 116, 117, 84, 83, 151, 133, 49, 152, 136, 176, 171, 157, 134, 113, 156, 135,
+    95, 96, 173, 174, 154, 155, 61, 50, 73, 38, 85, 74, 97, 62, 86, 180, 98,
 )
 
 
@@ -330,7 +327,8 @@
                                             device_id=peer(link), device_id_type=MESH)
 
     waited = set()
-    for name in ORDER:
+    names = list(plan.steps)
+    for name in (names[n] for n in ORDER):
         _, waits, _, _, work, sends = plan.steps[name]
         for one in waits:
             if one not in waited:
@@ -366,10 +364,10 @@
             pltpu.VMEM((KOUT, NOUT), BF16),
             pltpu.VMEM((TOKENS, NOUT), F32),
             pltpu.VMEM((TOKENS, NOUT), BF16),
-            pltpu.VMEM((2, 256, GCOL), F32),
-            pltpu.VMEM((2, 256, GCOL), BF16),
-            pltpu.VMEM((2, 6, 128, GCOL), BF16),
-            pltpu.VMEM((2, 6, 32, GCOL), BF16),
+            pltpu.VMEM((4, 256, GCOL), F32),
+            pltpu.VMEM((4, 256, GCOL), BF16),
+            pltpu.VMEM((4, 6, 128, GCOL), BF16),
+            pltpu.VMEM((4, 6, 32, GCOL), BF16),
             pltpu.SemaphoreType.DMA((count,)),
             pltpu.SemaphoreType.DMA((count,)),
             pltpu.SemaphoreType.DMA((12,)),
@@ -379,32 +377,39 @@
     )(activations, act_basis, grads, grad_basis)
 
 
-def square_kernel(rot, grad, out):
+def square_kernel(rot, grad, out, held, sem):
     row = lax.axis_index("row")
     x, y = row // 4, lax.rem(row, 4)
-    total = None
-    for i in range(4):
-        blocks = [(half, i, j) for half in "AB" for j in range(4)]
-        left = jnp.concatenate([rot[pl.ds(ROW[f"{h}{i}{j}"], 32), :] for h, i, j in blocks], axis=0)
-        right = []
-        for h, i, j in blocks:
-            token = (lax.rem(x + i, 4) * 4 + lax.rem(y + j, 4)) * 64 + (0 if h == "A" else 32)
-            right.append(grad[ds(token, 32, 32), :])
-        right = jnp.concatenate(right, axis=0)
-        products = lax.dot_general(left, right, (((0,), (0,)), ((), ())), preferred_element_type=F32)
-        total = products * products if total is None else total + products * products
-    out[...] = total * (1.0 / (LEN * SEQS))
+    order = [[(half, i, j) for half in "AB" for j in range(4)] for i in range(4)]
+
+    def token(h, i, j):
+        return (lax.rem(x + i, 4) * 4 + lax.rem(y + j, 4)) * 64 + (0 if h == "A" else 32)
+
+    tile, copies = 256, []
+    for r in range(0, NIN, tile):
+        left = [jnp.concatenate([rot[pl.ds(ROW[f"{h}{i}{j}"], 32), r : r + tile] for h, i, j in blocks], axis=0) for blocks in order]
+        for n in range(0, NOUT, tile):
+            total = None
+            for s, blocks in enumerate(order):
+                right = jnp.concatenate([grad[ds(token(h, i, j), 32, 32), n : n + tile] for h, i, j in blocks], axis=0)
+                products = lax.dot_general(left[s], right, (((0,), (0,)), ((), ())), preferred_element_type=F32)
+                total = products * products if total is None else total + products * products
+            held[r : r + tile, n : n + tile] = total * (1.0 / (LEN * SEQS))
+            where = (pl.ds(r, tile), pl.ds(n, tile))
+            copies.append(pltpu.make_async_copy(held.at[where], out.at[where], sem.at[len(copies)]))
+            copies[-1].start()
+    for one in copies:
+        one.wait()
 
 
 def square(rot, grad):
-    rows = 256
     return pl.pallas_call(
         square_kernel,
         out_shape=jax.ShapeDtypeStruct((NIN, NOUT), F32),
-        grid=(NIN // rows,),
-        in_specs=[pl.BlockSpec((TOKENS, rows), lambda i: (0, i)), pl.BlockSpec((TOKENS, NOUT), lambda i: (0, 0))],
-        out_specs=pl.BlockSpec((rows, NOUT), lambda i: (i, 0)),
-        compiler_params=pltpu.CompilerParams(dimension_semantics=("arbitrary",), vmem_limit_bytes=20 * 2**20),
+        in_specs=[pl.BlockSpec(memory_space=pltpu.VMEM)] * 2,
+        out_specs=pl.BlockSpec(memory_space=pl.ANY),
+        scratch_shapes=[pltpu.VMEM((NIN, NOUT), F32), pltpu.SemaphoreType.DMA((28,))],
+        compiler_params=pltpu.CompilerParams(vmem_limit_bytes=20 * 2**20),
         name="square",
     )(rot, grad)
 

time: 87.1 us -> 86.3 us (level)
  Pallas kernels: 86.9 us -> 86 us
    pallas_call x1, Pallas kernels: 7.06 us -> 5.09 us  [square(): pl.pallas_call(square_kernel, out_shape=jax.ShapeDtypeStruct((NIN, NOUT),...]
    pallas_call x1, Pallas kernels: 79.9 us -> 80.9 us  [rotate(): pl.pallas_call(lambda *refs: rotate_kernel(plan, *refs), out_shape=[pltpu...]
where the time goes in v3:
time: 86.3 us; the launch traced here: 86.2 us
  Pallas kernels  86 us (100%)
    pallas_call x1, Pallas kernels, rotate(): pl.pallas_call(lambda *refs: rotate_kernel(plan, *refs), out_shape=[pltpu...  80.9 us
    pallas_call x1, Pallas kernels, square(): pl.pallas_call(square_kernel, out_shape=jax.ShapeDtypeStruct((NIN, NOUT),...  5.09 us

profile of v3, /device:TPU:1, one launch (start us, length us, event | category | flops | bytes accessed | tf_op | source)
XLA Modules:
  0.0 86.2 jit_solution(4833008033776567765)
XLA Ops:
  0.0 80.9 %rotate.1 = (bf16[1024,1792]{1,0:T(8,128)(2,1)S(1)}, bf16[1024,1024]{1,0:T(8,128)(2,1)S(1)}) custom-call(bf16[64,3584]{1,0:T(8,128)(2,1)} %refs_0_.1, bf16[3584,1792]{1,0:T(8,128)(2,1)} %refs_1_.1, bf16[128,512]{1,0:T(8,128)(2,1)} %refs_2_.1, bf16[512,1024]{1,0:T(8,128)(2,1)} %refs_3_.1), custom_call_target="tpu_custom_call" | custom-call | tf_op jit(solution)/shard_map/rotate/pallas_call | solution.py:351
  81.0 5.1 %square.1 = f32[1792,1024]{1,0:T(8,128)} custom-call(bf16[1024,1792]{1,0:T(8,128)(2,1)S(1)} %get-tuple-element.7.rot, bf16[1024,1024]{1,0:T(8,128)(2,1)S(1)} %get-tuple-element.8.grad), custom_call_target="tpu_custom_call" | custom-call | tf_op jit(solution)/shard_map/square/pallas_call | solution.py:406
